TPU v7x, 128 devices: a whole 4x4x4 slice. The times are simulated.
128 devices in a mesh: member: 32 (over x, y, core), lat: 4 (over z).
Axes of the slice: x: 4, y: 4, z: 4, core: 2. Of those that a mesh axis runs over, the one named last changes fastest.
Arguments:
- ensemble: float32 [64, 3, 1, 128, 1440], P('member', None, None, 'lat'), may hold values from -6 to 6
- observation: float32 [3, 1, 128, 1440], P(None, None, 'lat'), may hold values from -6 to 6
- valid_mask: int32 [64], P('member'), may hold values from 0 to 1, as said below
- band_start: int32 [4], P('lat'), may hold values from 0 to 689
Outputs:
- crps_field: float32 [3, 1, 128, 1440], P(None, None, ('lat', 'member'))
- score_table: float32 [3, 1], replicated
Inputs may be any that keep to these rules, and one draw needn't show every extreme that they name: `valid_mask`: exactly 50 entries are 1, at positions drawn afresh.
All inputs are finite; a program needn't handle non-finite values.
Results may differ from a plain program's by a relative error of at most 0.0001.
Values sent between devices are 32-bit elements; how exact they have to be, the bound alone decides.
No kernel may reach another device: no remote copies, remote signals or barrier semaphores. Data moves between devices by JAX's collectives and lax.ppermute only.
A program may use at most 64 MiB of HBM per device.

v0:
```python
import functools
import math

import jax
import jax.numpy as jnp
from jax import lax
from jax.sharding import Mesh
from jax.sharding import PartitionSpec as P

GRID_LAT = 721
GRID_LON = 1440
MEMBER = ("member_0", "member_1", "member_2")
MEMBER_LAT = ("member_0", "member_1", "member_2", "lat")
LAT_MEMBER = ("lat", "member_0", "member_1", "member_2")


def sent_to_all(x, axis):
    copies = jnp.broadcast_to(x, (lax.axis_size(axis), *x.shape))
    return lax.all_to_all(copies, axis, split_axis=0, concat_axis=0, tiled=True)


def laid_out(parts, dim):
    parts = jnp.moveaxis(parts, 0, dim)
    dims = parts.shape
    return parts.reshape(*dims[:dim], dims[dim] * dims[dim + 1], *dims[dim + 2 :])


def collect(x, axis, dim):
    parts = sent_to_all(x, axis)
    return laid_out(parts, dim)


def by_axis(x, axes):
    return functools.reduce(lax.psum, axes, x)


def on_device(ensemble, observation, valid_mask, band_start):
    member_flags = valid_mask.astype(jnp.float32)
    lat_rows = ensemble.shape[3]
    block_rows = lat_rows // lax.axis_size(MEMBER)
    row_offset = lax.axis_index(MEMBER) * block_rows
    members = lax.all_to_all(ensemble, MEMBER, split_axis=3, concat_axis=0, tiled=True)
    all_flags = collect(member_flags, MEMBER, 0)
    slot_total = members.shape[0]
    truth_slice = lax.dynamic_slice_in_dim(observation, row_offset, block_rows, 2)
    valid_count = jnp.sum(all_flags)
    flag_column = all_flags[:, None, None, None, None]
    skill_term = jnp.sum(flag_column * jnp.abs(members - truth_slice[None]), axis=0)
    group_count = slot_total // 8
    blocks = members.reshape((group_count, 8) + members.shape[1:])
    block_flags = all_flags.reshape(group_count, 8)

    def block_sum(block_item):
        block_slab, flags_here = block_item

        def add_one(position, running_sum):
            one_slab = lax.dynamic_index_in_dim(block_slab, position, 0, keepdims=True)
            one_flag = lax.dynamic_index_in_dim(flags_here, position, 0, keepdims=False)
            return running_sum + one_flag * jnp.sum(
                flag_column * jnp.abs(one_slab - members), axis=0
            )

        return lax.fori_loop(0, 8, add_one, jnp.zeros(truth_slice.shape, jnp.float32))

    spread = jnp.sum(lax.map(block_sum, (blocks, block_flags)), axis=0)
    crps_field = skill_term / valid_count - spread / (2.0 * valid_count * (valid_count - 1.0))
    row_index = (band_start[0] + row_offset + jnp.arange(block_rows, dtype=jnp.int32)).astype(
        jnp.float32
    )
    weight = jnp.cos((90.0 - row_index * 180.0 / (GRID_LAT - 1)) * math.pi / 180.0)
    partial_sums = jnp.sum(crps_field * weight[:, None], axis=(2, 3))
    totals = by_axis(partial_sums, MEMBER_LAT)
    score_table = totals / (lax.axis_size("lat") * lat_rows * GRID_LON)
    return (crps_field, score_table)


def solution(mesh):
    torus = Mesh(
        mesh.devices.reshape(4, 4, 2, mesh.shape["lat"]),
        ("member_0", "member_1", "member_2", "lat"),
    )
    in_specs = (P(MEMBER, None, None, "lat", None), P(None, None, "lat", None), P(MEMBER), P("lat"))
    out_specs = (P(None, None, LAT_MEMBER, None), P())
    return jax.shard_map(
        on_device, mesh=torus, in_specs=in_specs, out_specs=out_specs, check_vma=False
    )
```

profile of v0, /device:TPU:1, one launch (start us, length us, event | category | flops | bytes accessed | tf_op | source)
XLA Modules:
  0.0 281.1 jit_solution(1610681111426072009)
XLA Ops:
  2.0 8.6 %all-to-all-start = ((f32[32,1,2]{2,1,0:T(1,128)}), f32[32,1,2]{2,1,0:T(1,128)S(1)}, u32[]{:S(2)}, u32[]{:S(2)}) async-start(f32[32,1,2]{2,1,0:T(1,128)} %broadcast_in_dim.11), calls=%async_computation | async-start | bytes 32768 | tf_op jit(solution)/shard_map/all_to_all | solution.py:19
  10.6 3.2 %copy.28 = f32[2,3,1,32,1440]{4,1,2,0,3:T(4,128)} copy(f32[2,3,1,32,1440]{4,3,2,1,0:T(8,128)} %param.8) | data formatting | bytes 2211840 | tf_op args[0]
  13.8 3.7 %all-to-all-done = f32[32,1,2]{2,1,0:T(1,128)S(1)} async-done(((f32[32,1,2]{2,1,0:T(1,128)}), f32[32,1,2]{2,1,0:T(1,128)S(1)}, u32[]{:S(2)}, u32[]{:S(2)}) %all-to-all-start) | async-done | bytes 288 | tf_op jit(solution)/shard_map/all_to_all | solution.py:19
  17.5 4.3 %all-to-all-start.1 = ((f32[2,3,1,32,1440]{4,1,2,0,3:T(4,128)}), f32[2,3,1,32,1440]{4,1,2,0,3:T(4,128)S(1)}, u32[]{:S(2)}, u32[]{:S(2)}) async-start(f32[2,3,1,32,1440]{4,1,2,0,3:T(4,128)} %copy.28), calls=%async_computation.1 | async-start | bytes 3145728 | tf_op jit(solution)/shard_map/all_to_all | solution.py:42
  25.9 18.6 %all-to-all-done.1 = f32[2,3,1,32,1440]{4,1,2,0,3:T(4,128)S(1)} async-done(((f32[2,3,1,32,1440]{4,1,2,0,3:T(4,128)}), f32[2,3,1,32,1440]{4,1,2,0,3:T(4,128)S(1)}, u32[]{:S(2)}, u32[]{:S(2)}) %all-to-all-start.1) | async-done | bytes 1105952 | tf_op jit(solution)/shard_map/all_to_all | solution.py:42
  46.5 202.5 %while.25 = (s32[]{:T(128)}, f32[8,3,1,1,1440]{4,3,2,1,0:T(1,128)S(1)}, f32[8,8,3,1,1,1440]{5,4,3,2,1,0:T(1,128)S(1)}, f32[8,8]{1,0:T(8,128)S(1)}, f32[64,1,1,1,...) while((s32[]{:T(128)}, ...), condition=%wide.region_6.7_spmd, body=%wide.region_2.6_spmd.sunk | while | flops 1114565 | bytes 1609964 | solution.py:65
  46.6 25.2 %while.26 = (s32[]{:T(128)}, f32[3,1,1,1440]{3,2,1,0:T(1,128)S(1)}, f32[8]{0:T(128)S(1)}, f32[64,1,1,1,1]{0,4,3,2,1:T(1,128)S(1)}, f32[8,3,1,1,1440]{4,3,2,1,0:T...) while((s32[]{:T(128)}, f32[3,1,1,1440]{3,2,1,0:T(1,128)S(1)}, ...), condition=%wide.region_5.5_spmd.clone, body=%wide.region_3.4_spmd.clone.sunk | while | flops 1114563 | bytes 1296371 | solution.py:63
  52.9 1.7 multiply_reduce_fusion.4
  62.4 1.7 multiply_reduce_fusion.4
  65.6 1.7 multiply_reduce_fusion.4
  71.9 25.2 %while.26 = (s32[]{:T(128)}, f32[3,1,1,1440]{3,2,1,0:T(1,128)S(1)}, f32[8]{0:T(128)S(1)}, f32[64,1,1,1,1]{0,4,3,2,1:T(1,128)S(1)}, f32[8,3,1,1,1440]{4,3,2,1,0:T...) while((s32[]{:T(128)}, f32[3,1,1,1440]{3,2,1,0:T(1,128)S(1)}, ...), condition=%wide.region_5.5_spmd.clone, body=%wide.region_3.4_spmd.clone.sunk | while | flops 1114563 | bytes 1296371 | solution.py:63
  75.1 1.7 multiply_reduce_fusion.4
  78.3 1.7 multiply_reduce_fusion.4
  87.7 1.7 multiply_reduce_fusion.4
  97.2 25.2 %while.26 = (s32[]{:T(128)}, f32[3,1,1,1440]{3,2,1,0:T(1,128)S(1)}, f32[8]{0:T(128)S(1)}, f32[64,1,1,1,1]{0,4,3,2,1:T(1,128)S(1)}, f32[8,3,1,1,1440]{4,3,2,1,0:T...) while((s32[]{:T(128)}, f32[3,1,1,1440]{3,2,1,0:T(1,128)S(1)}, ...), condition=%wide.region_5.5_spmd.clone, body=%wide.region_3.4_spmd.clone.sunk | while | flops 1114563 | bytes 1296371 | solution.py:63
  122.5 25.2 %while.26 = (s32[]{:T(128)}, f32[3,1,1,1440]{3,2,1,0:T(1,128)S(1)}, f32[8]{0:T(128)S(1)}, f32[64,1,1,1,1]{0,4,3,2,1:T(1,128)S(1)}, f32[8,3,1,1,1440]{4,3,2,1,0:T...) while((s32[]{:T(128)}, f32[3,1,1,1440]{3,2,1,0:T(1,128)S(1)}, ...), condition=%wide.region_5.5_spmd.clone, body=%wide.region_3.4_spmd.clone.sunk | while | flops 1114563 | bytes 1296371 | solution.py:63
  147.9 25.2 %while.26 = (s32[]{:T(128)}, f32[3,1,1,1440]{3,2,1,0:T(1,128)S(1)}, f32[8]{0:T(128)S(1)}, f32[64,1,1,1,1]{0,4,3,2,1:T(1,128)S(1)}, f32[8,3,1,1,1440]{4,3,2,1,0:T...) while((s32[]{:T(128)}, f32[3,1,1,1440]{3,2,1,0:T(1,128)S(1)}, ...), condition=%wide.region_5.5_spmd.clone, body=%wide.region_3.4_spmd.clone.sunk | while | flops 1114563 | bytes 1296371 | solution.py:63
  173.2 25.2 %while.26 = (s32[]{:T(128)}, f32[3,1,1,1440]{3,2,1,0:T(1,128)S(1)}, f32[8]{0:T(128)S(1)}, f32[64,1,1,1,1]{0,4,3,2,1:T(1,128)S(1)}, f32[8,3,1,1,1440]{4,3,2,1,0:T...) while((s32[]{:T(128)}, f32[3,1,1,1440]{3,2,1,0:T(1,128)S(1)}, ...), condition=%wide.region_5.5_spmd.clone, body=%wide.region_3.4_spmd.clone.sunk | while | flops 1114563 | bytes 1296371 | solution.py:63
  198.5 25.2 %while.26 = (s32[]{:T(128)}, f32[3,1,1,1440]{3,2,1,0:T(1,128)S(1)}, f32[8]{0:T(128)S(1)}, f32[64,1,1,1,1]{0,4,3,2,1:T(1,128)S(1)}, f32[8,3,1,1,1440]{4,3,2,1,0:T...) while((s32[]{:T(128)}, f32[3,1,1,1440]{3,2,1,0:T(1,128)S(1)}, ...), condition=%wide.region_5.5_spmd.clone, body=%wide.region_3.4_spmd.clone.sunk | while | flops 1114563 | bytes 1296371 | solution.py:63
  223.8 25.2 %while.26 = (s32[]{:T(128)}, f32[3,1,1,1440]{3,2,1,0:T(1,128)S(1)}, f32[8]{0:T(128)S(1)}, f32[64,1,1,1,1]{0,4,3,2,1:T(1,128)S(1)}, f32[8,3,1,1,1440]{4,3,2,1,0:T...) while((s32[]{:T(128)}, f32[3,1,1,1440]{3,2,1,0:T(1,128)S(1)}, ...), condition=%wide.region_5.5_spmd.clone, body=%wide.region_3.4_spmd.clone.sunk | while | flops 1114563 | bytes 1296371 | solution.py:63
  250.0 6.6 %psum.28 = f32[3,1]{0,1:T(1,128)S(1)} all-reduce(f32[3,1]{0,1:T(1,128)S(1)} %bitcast.51), channel_id=1, replica_groups=mesh['member_0'=4,'member_1'=4,'member_2'=2,'lat'=4] {'member_0'}, use_global_device_ids=true, to_apply=%region_9.10 | all-reduce | flops 3 | bytes 24 | tf_op jit(solution)/shard_map/psum | solution.py:34
  256.6 7.2 %psum.29 = f32[3,1]{0,1:T(1,128)S(1)} all-reduce(f32[3,1]{0,1:T(1,128)S(1)} %psum.28), channel_id=1, replica_groups=mesh['member_0'=4,'member_1'=4,'member_2'=2,'lat'=4] {'member_1'}, use_global_device_ids=true, to_apply=%region_10.11 | all-reduce | flops 3 | bytes 24 | tf_op jit(solution)/shard_map/psum | solution.py:34
  263.7 6.5 %psum.30 = f32[3,1]{0,1:T(1,128)S(1)} all-reduce(f32[3,1]{0,1:T(1,128)S(1)} %psum.29), channel_id=1, replica_groups=mesh['member_0'=4,'member_1'=4,'member_2'=2,'lat'=4] {'member_2'}, use_global_device_ids=true, to_apply=%region_11.12 | all-reduce | flops 3 | bytes 24 | tf_op jit(solution)/shard_map/psum | solution.py:34
  270.8 9.7 %psum.31 = f32[3,1]{0,1:T(1,128)S(1)} all-reduce(f32[3,1]{0,1:T(1,128)S(1)} %psum.30), channel_id=1, replica_groups=mesh['member_0'=4,'member_1'=4,'member_2'=2,'lat'=4] {'lat'}, use_global_device_ids=true, to_apply=%region_12.13 | all-reduce | flops 3 | bytes 24 | tf_op jit(solution)/shard_map/psum | solution.py:34
  (428 shorter events, 197.0 us)
Async XLA Ops:
  0.6 21.1 %copy-start = (f32[3,1,32,1440]{3,2,1,0:T(8,128)S(1)}, f32[3,1,32,1440]{3,2,1,0:T(8,128)}, u32[]{:S(2)}) copy-start(f32[3,1,32,1440]{3,2,1,0:T(8,128)} %param.9) | copy-start | bytes 1658884
  2.0 15.5 %all-to-all-start = ((f32[32,1,2]{2,1,0:T(1,128)}), f32[32,1,2]{2,1,0:T(1,128)S(1)}, u32[]{:S(2)}, u32[]{:S(2)}) async-start(f32[32,1,2]{2,1,0:T(1,128)} %broadcast_in_dim.11), calls=%async_computation | async-start | bytes 32768 | tf_op jit(solution)/shard_map/all_to_all | solution.py:19
  17.5 27.0 %all-to-all-start.1 = ((f32[2,3,1,32,1440]{4,1,2,0,3:T(4,128)}), f32[2,3,1,32,1440]{4,1,2,0,3:T(4,128)S(1)}, u32[]{:S(2)}, u32[]{:S(2)}) async-start(f32[2,3,1,32,1440]{4,1,2,0,3:T(4,128)} %copy.28), calls=%async_computation.1 | async-start | bytes 3145728 | tf_op jit(solution)/shard_map/all_to_all | solution.py:42
where the time goes:
time: 283 us; the launch traced here: 281 us
  other arithmetic  160 us (57%)
  local copies, waits for them, and re-layouts  50.6 us (18%)
  blocking collectives  29.9 us (11%)
  waiting for transfers between devices  22.2 us (8%)
  starting transfers between devices  12.9 us (5%)
  loops' own time  2.88 us (1%)
    reduce_sum x64, other arithmetic, add_one(): jnp.sum(flag_column * jnp.abs(one_slab - members), axis=0)  108 us
    mul x64, other arithmetic, add_one(): one_flag * jnp.sum(flag_column * jnp.abs(one_slab - members), axis=0)  44.4 us
    dynamic_slice x64, local copies, waits for them, and re-layouts, add_one(): one_flag = lax.dynamic_index_in_dim(flags_here, position, 0, keepdims=False)  42.6 us
    psum x4, blocking collectives, by_axis(): return functools.reduce(lax.psum, axes, x)  29.9 us
    all_to_all x1, waiting for transfers between devices, on_device(): lax.all_to_all(ensemble, MEMBER, split_axis=3, concat_axis=0, tiled=True)  18.6 us
    all_to_all x1, starting transfers between devices, sent_to_all(): return lax.all_to_all(copies, axis, split_axis=0, concat_axis=0, tiled=True)  8.58 us
  transfers between devices with their start and end apart: 2, of which 2 were waited for; matrix products, arithmetic and copies ran while one was open for 2% of the time, Pallas kernels for 0%

commit v1 on v0

v1 whole, which is shorter than its diff:
```python
import math

import jax
import jax.numpy as jnp
from jax import lax
from jax.experimental import pallas as pl
from jax.experimental.pallas import tpu as pltpu
from jax.sharding import Mesh
from jax.sharding import PartitionSpec as P

GRID_LAT = 721
GRID_LON = 1440
LANES = 128
COLS = 12
VARS = 3
ROWS = 36
BLOCK = 72
MEMBERS = 64
VALID = 50
VMEM_LIMIT = 8 * 2**20
PAD = 1e30
MEMBER = ("member_0", "member_1", "member_2")
MEMBER_LAT = ("member_0", "member_1", "member_2", "lat")
LAT_MEMBER = ("lat", "member_0", "member_1", "member_2")


def slot(member, row):
    return 32 * member + row if row < 32 else 64 + 4 * member + row - 32


def pack_kernel(mask_ref, in_ref, out_ref):
    for member in range(2):
        valid = mask_ref[member] != 0
        for var in range(VARS):
            for col in range(COLS):
                low = col * LANES
                high = min(low + LANES, GRID_LON)
                piece = in_ref[member * VARS + var, :, low:high]
                if high - low < LANES:
                    fill = jnp.zeros((8, LANES - (high - low)), jnp.float32)
                    piece = jnp.concatenate([piece, fill], axis=1)
                piece = jnp.where(valid, piece, PAD)
                row = slot(member, var * COLS + col)
                out_ref[pl.ds(row, 8, stride=BLOCK), :] = piece


def pack(ensemble, valid_mask):
    rows = ensemble.shape[3]
    flat = ensemble.reshape(2 * VARS, rows, GRID_LON)
    packed = pl.pallas_call(
        pack_kernel,
        grid=(rows // 8,),
        in_specs=[
            pl.BlockSpec(memory_space=pltpu.SMEM),
            pl.BlockSpec((2 * VARS, 8, GRID_LON), lambda t: (0, t, 0)),
        ],
        out_specs=pl.BlockSpec((8 * BLOCK, LANES), lambda t: (t, 0)),
        out_shape=jax.ShapeDtypeStruct((rows * BLOCK, LANES), jnp.float32),
        name="pack",
    )(valid_mask, flat)
    return packed.reshape(rows, BLOCK, LANES)


def truth_kernel(row_ref, in_ref, out_ref):
    mine = lax.broadcasted_iota(jnp.int32, (8, LANES), 0) == row_ref[0] % 8
    out_ref[...] = jnp.zeros(out_ref.shape, jnp.float32)
    for var in range(VARS):
        for col in range(COLS):
            low = col * LANES
            high = min(low + LANES, GRID_LON)
            piece = jnp.where(mine[:, : high - low], in_ref[var, :, low:high], 0.0)
            row = var * COLS + col
            out_ref[row : row + 1, : high - low] = jnp.sum(piece, axis=0, keepdims=True)


def truth(observation, row):
    flat = observation.reshape(VARS, observation.shape[2], GRID_LON)
    return pl.pallas_call(
        truth_kernel,
        grid_spec=pltpu.PrefetchScalarGridSpec(
            num_scalar_prefetch=1,
            grid=(1,),
            in_specs=[pl.BlockSpec((VARS, 8, GRID_LON), lambda i, where: (0, where[0] // 8, 0))],
            out_specs=pl.BlockSpec((40, LANES), lambda i, where: (0, 0)),
        ),
        out_shape=jax.ShapeDtypeStruct((40, LANES), jnp.float32),
        compiler_params=pltpu.CompilerParams(vmem_limit_bytes=VMEM_LIMIT),
        name="truth",
    )(row.reshape(1), flat)


def compare(values, i, j):
    low, high = values[i], values[j]
    values[i] = jnp.minimum(low, high)
    values[j] = jnp.maximum(low, high)


def merge(values, where):
    if len(where) == 2:
        compare(values, where[0], where[1])
        return
    merge(values, where[0::2])
    merge(values, where[1::2])
    for k in range(1, len(where) - 1, 2):
        compare(values, where[k], where[k + 1])


def sort(values, where):
    if len(where) == 1:
        return
    half = len(where) // 2
    sort(values, where[:half])
    sort(values, where[half:])
    merge(values, where)


def score_of(ordered, observed):
    skill = sum(jnp.abs(v - observed) for v in ordered)
    spread = sum(
        (VALID - 1.0 - 2 * k) * (ordered[VALID - 1 - k] - ordered[k]) for k in range(VALID // 2)
    )
    return skill * (1.0 / VALID) - spread * (1.0 / (VALID * (VALID - 1.0)))


def score_kernel(weight_ref, in_ref, truth_ref, field_ref, sums_ref, field):
    @pl.loop(0, 4)
    def _(tile):
        start = pl.multiple_of(tile * 8, 8)
        values = []
        for source in range(MEMBERS // 2):
            values.append(in_ref[source, pl.ds(start, 8), :])
            values.append(in_ref[source, pl.ds(32 + start, 8), :])
        sort(values, list(range(MEMBERS)))
        field[pl.ds(start, 8), :] = score_of(values[:VALID], truth_ref[pl.ds(start, 8), :])

    half = MEMBERS // 2
    values = [in_ref[source, 64:72, :] for source in range(half)]
    sort(values, list(range(half)))
    upper = lax.broadcasted_iota(jnp.int32, (8, LANES), 0) >= 4
    other = [pltpu.roll(v, 4, 0) for v in values]
    values = [
        jnp.where(
            upper,
            jnp.maximum(values[k], other[half - 1 - k]),
            jnp.minimum(values[k], other[half - 1 - k]),
        )
        for k in range(half)
    ]
    step = half // 2
    while step:
        for k in range(half):
            if not k & step:
                compare(values, k, k + step)
        step //= 2
    above = [pltpu.roll(v, 4, 0) for v in values[: VALID - half]]
    field[32:40, :] = score_of(values + above, truth_ref[32:40, :])

    lane = lax.broadcasted_iota(jnp.int32, (1, LANES), 1)
    last = GRID_LON - (COLS - 1) * LANES
    sums = jnp.zeros((1, LANES), jnp.float32)
    for var in range(VARS):
        total = jnp.zeros((1, LANES), jnp.float32)
        for col in range(COLS):
            row = field[var * COLS + col : var * COLS + col + 1, :]
            low = col * LANES
            if col == COLS - 1:
                field_ref[var, :, low:GRID_LON] = row[:, :last]
                row = jnp.where(lane < last, row, 0.0)
            else:
                field_ref[var, :, low : low + LANES] = row
            total = total + row
        total = jnp.sum(total, axis=1, keepdims=True)
        sums = jnp.where(lane == var, total, sums)
    sums_ref[...] = jnp.broadcast_to(sums * weight_ref[0], sums_ref.shape)


def score(weight, members, observed, copies):
    return pl.pallas_call(
        score_kernel,
        in_specs=[
            pl.BlockSpec(memory_space=pltpu.SMEM),
            pl.BlockSpec(memory_space=pltpu.VMEM),
            pl.BlockSpec(memory_space=pltpu.VMEM),
        ],
        out_specs=[pl.BlockSpec(memory_space=pltpu.VMEM)] * 2,
        out_shape=[
            jax.ShapeDtypeStruct((VARS, 1, GRID_LON), jnp.float32),
            jax.ShapeDtypeStruct((copies, LANES), jnp.float32),
        ],
        scratch_shapes=[pltpu.VMEM((40, LANES), jnp.float32)],
        compiler_params=pltpu.CompilerParams(vmem_limit_bytes=VMEM_LIMIT),
        name="score",
    )(weight, members, observed)


def on_device(ensemble, observation, valid_mask, band_start):
    lat_rows = ensemble.shape[3]
    row = lax.axis_index(MEMBER).astype(jnp.int32)
    packed = pack(ensemble, valid_mask)
    members = lax.all_to_all(packed, MEMBER, split_axis=0, concat_axis=0, tiled=True)
    observed = truth(observation, row)
    place = (band_start + row).astype(jnp.float32)
    weight = jnp.cos((90.0 - place * 180.0 / (GRID_LAT - 1)) * math.pi / 180.0)
    copies = lax.axis_size(MEMBER_LAT)
    field, sums = score(weight, members, observed, copies)
    sums = lax.all_to_all(sums, MEMBER_LAT, split_axis=0, concat_axis=0, tiled=True)
    total = jnp.sum(sums, axis=0)[:VARS].reshape(VARS, 1)
    score_table = total / (lax.axis_size("lat") * lat_rows * GRID_LON)
    return (field.reshape(VARS, 1, 1, GRID_LON), score_table)


def solution(mesh):
    torus = Mesh(
        mesh.devices.reshape(4, 4, 2, mesh.shape["lat"]),
        ("member_0", "member_1", "member_2", "lat"),
    )
    in_specs = (P(MEMBER, None, None, "lat", None), P(None, None, "lat", None), P(MEMBER), P("lat"))
    out_specs = (P(None, None, LAT_MEMBER, None), P())
    return jax.shard_map(
        on_device, mesh=torus, in_specs=in_specs, out_specs=out_specs, check_vma=False
    )
```

time: 283 us -> 50 us (0.18)
  other arithmetic: 160 us -> 0.67 us
  local copies, waits for them, and re-layouts: 50.6 us -> 0.01 us
  blocking collectives: 29.9 us -> 16.3 us
  Pallas kernels: 0 us -> 5.05 us
  waiting for transfers between devices: 22.2 us -> 17.6 us
  starting transfers between devices: 12.9 us -> 8.71 us
  loops' own time: 2.88 us -> 0 us
    reduce_sum x68 -> x1, other arithmetic: 111 us -> 0.15 us  [on_device(): total = jnp.sum(sums, axis=0)[:VARS].reshape(VARS, 1)]
    mul x64 -> x0, other arithmetic: 44.4 us -> none  [add_one(): one_flag * jnp.sum(flag_column * jnp.abs(one_slab - members), axis=0)]
    dynamic_slice x129 -> x0, local copies, waits for them, and re-layouts: 43.2 us -> none  [the longest x64 42.6 us: add_one(): one_flag = lax.dynamic_index_in_dim(flags_here, position, 0, keepdims=False)]
    psum x4 -> x0, blocking collectives: 29.9 us -> none  [by_axis(): return functools.reduce(lax.psum, axes, x)]
    all_to_all x0 -> x1, blocking collectives: none -> 16.3 us  [on_device(): lax.all_to_all(sums, MEMBER_LAT, split_axis=0, concat_axis=0, tiled=True)]
    pallas_call x0 -> x3, Pallas kernels: none -> 5.05 us  [the longest x1 3.5 us: pack(): pl.pallas_call(pack_kernel, grid=(rows // 8,), in_specs=[pl.BlockSpec(mem...]
    all_to_all x2 -> x1, waiting for transfers between devices: 22.2 us -> 17.6 us  [on_device(): lax.all_to_all(packed, MEMBER, split_axis=0, concat_axis=0, tiled=True)]
    all_to_all x2 -> x1, starting transfers between devices: 12.9 us -> 8.71 us  [on_device(): lax.all_to_all(packed, MEMBER, split_axis=0, concat_axis=0, tiled=True)]
  transfers between devices with their start and end apart: 2 -> 1, of which waited for: 2 -> 1; matrix products, arithmetic and copies ran while one was open for 2% -> 0% of each run, Pallas kernels for 0% -> 0%
where the time goes in v1:
time: 50 us; the launch traced here: 49.7 us
  waiting for transfers between devices  17.6 us (35%)
  blocking collectives  16.3 us (33%)
  starting transfers between devices  8.71 us (17%)
  Pallas kernels  5.05 us (10%)
  between operations  1.39 us (3%)
  other arithmetic  0.67 us (1%)
    all_to_all x1, waiting for transfers between devices, on_device(): lax.all_to_all(packed, MEMBER, split_axis=0, concat_axis=0, tiled=True)  17.6 us
    all_to_all x1, blocking collectives, on_device(): lax.all_to_all(sums, MEMBER_LAT, split_axis=0, concat_axis=0, tiled=True)  16.3 us
    all_to_all x1, starting transfers between devices, on_device(): lax.all_to_all(packed, MEMBER, split_axis=0, concat_axis=0, tiled=True)  8.71 us
    pallas_call x1, Pallas kernels, pack(): pl.pallas_call(pack_kernel, grid=(rows // 8,), in_specs=[pl.BlockSpec(mem...  3.5 us
    pallas_call x1, Pallas kernels, score(): pl.pallas_call(score_kernel, in_specs=[pl.BlockSpec(memory_space=pltpu.SM...  1.5 us
  transfers between devices with their start and end apart: 1, of which 1 were waited for; matrix products, arithmetic and copies ran while one was open for 0% of the time, Pallas kernels for 0%

profile of v1, /device:TPU:1, one launch (start us, length us, event | category | flops | bytes accessed | tf_op | source)
XLA Modules:
  0.0 49.7 jit_solution(13225975117555739329)
XLA Ops:
  0.6 3.5 %pack.1 = f32[2304,128]{1,0:T(8,128)} custom-call(s32[2]{0:T(128)} %mask_ref.1, f32[6,32,1440]{2,1,0:T(8,128)} %bitcast.15), custom_call_target="tpu_custom_call" | custom-call | tf_op jit(solution)/shard_map/pack/pallas_call | solution.py:50
  4.1 0.0 copy-start
  4.1 8.7 %all-to-all-start = ((f32[32,72,128]{2,1,0:T(8,128)}), f32[32,72,128]{2,1,0:T(8,128)S(1)}, u32[]{:S(2)}, u32[]{:S(2)}) async-start(f32[32,72,128]{2,1,0:T(8,128)} %bitcast.14), calls=%async_computation | async-start | bytes 2359296 | tf_op jit(solution)/shard_map/all_to_all | solution.py:200
  13.6 0.0 copy-done
  13.6 17.6 %all-to-all-done.in_ref = f32[32,72,128]{2,1,0:T(8,128)S(1)} async-done(((f32[32,72,128]{2,1,0:T(8,128)}), f32[32,72,128]{2,1,0:T(8,128)S(1)}, u32[]{:S(2)}, u32[]{:S(2)}) %all-to-all-start) | async-done | bytes 1179680 | tf_op jit(solution)/shard_map/all_to_all | solution.py:200
  31.2 1.5 %score.1 = (f32[3,1,1440]{2,1,0:T(1,128)}, f32[128,128]{1,0:T(8,128)S(1)}) custom-call(f32[1]{0:T(128)S(6)} %cos.3.weight_ref, f32[32,72,128]{2,1,0:T(8,128)S(1)} %all-to-all-done.in_ref, f32[40,128]{1,0:T(8,128)S(1)} %truth.1.truth_ref), custom_call_target="tpu_custom_call" | custom-call | tf_op jit(solution)/shard_map/score/pallas_call | solution.py:178
  32.7 16.3 %all_to_all.14 = f32[128,1,128]{2,1,0:T(1,128)S(1)} all-to-all(f32[128,1,128]{2,1,0:T(1,128)S(1)} %bitcast.13), channel_id=1, replica_groups=mesh['member_0'=4,'member_1'=4,'member_2'=2,'lat'=4] {'member_0','member..., dimensions={0} | all-to-all | bytes 131072 | tf_op jit(solution)/shard_map/all_to_all | solution.py:206
  49.0 0.2 reduce_sum.9
  49.2 0.5 %multiply_bitcast_fusion = f32[3,1]{0,1:T(1,128)} fusion(f32[128]{0:T(128)S(1)} %reduce_sum.9), kind=kLoop, calls=%fused_computation | loop fusion | flops 3 | bytes 24 | tf_op jit(solution)/shard_map/div | solution.py:208
  (1 shorter events, 0.0 us)
Async XLA Ops:
  4.1 9.5 %copy-start = (f32[3,1,32,1440]{3,2,1,0:T(8,128)S(1)}, f32[3,1,32,1440]{3,2,1,0:T(8,128)}, u32[]{:S(2)}) copy-start(f32[3,1,32,1440]{3,2,1,0:T(8,128)} %param.5) | copy-start | bytes 1658884
  4.1 27.1 %all-to-all-start = ((f32[32,72,128]{2,1,0:T(8,128)}), f32[32,72,128]{2,1,0:T(8,128)S(1)}, u32[]{:S(2)}, u32[]{:S(2)}) async-start(f32[32,72,128]{2,1,0:T(8,128)} %bitcast.14), calls=%async_computation | async-start | bytes 2359296 | tf_op jit(solution)/shard_map/all_to_all | solution.py:200

commit v2 on v1

--- a/solution.py
+++ b/solution.py
@@ -1,3 +1,4 @@
+import functools
 import math
 
 import jax
@@ -28,65 +29,113 @@
     return 32 * member + row if row < 32 else 64 + 4 * member + row - 32
 
 
-def pack_kernel(mask_ref, in_ref, out_ref):
-    for member in range(2):
-        valid = mask_ref[member] != 0
-        for var in range(VARS):
-            for col in range(COLS):
-                low = col * LANES
-                high = min(low + LANES, GRID_LON)
-                piece = in_ref[member * VARS + var, :, low:high]
-                if high - low < LANES:
-                    fill = jnp.zeros((8, LANES - (high - low)), jnp.float32)
-                    piece = jnp.concatenate([piece, fill], axis=1)
-                piece = jnp.where(valid, piece, PAD)
-                row = slot(member, var * COLS + col)
-                out_ref[pl.ds(row, 8, stride=BLOCK), :] = piece
+def position():
+    return lax.axis_index(MEMBER).astype(jnp.int32)
+
+
+def in_hbm(x):
+    return pltpu.with_memory_space_constraint(x, pltpu.HBM)
+
+
+def pack_kernel(mask_in, in_ref, out_ref, mask_ref, held, packed, arrived, left):
+    tiles = held.shape[1] // 8
+    depth = 8 * BLOCK
+
+    def bring(tile):
+        rows = pl.ds(tile * 8, 8)
+        return pltpu.make_async_copy(
+            in_ref.at[:, rows, :], held.at[:, rows, :], arrived.at[tile]
+        )
+
+    def take(tile):
+        rows = pl.ds(tile * depth, depth)
+        return pltpu.make_async_copy(packed.at[rows, :], out_ref.at[rows, :], left.at[tile])
+
+    flags = pltpu.make_async_copy(mask_in, mask_ref, arrived.at[tiles])
+    flags.start()
+    for tile in range(tiles):
+        bring(tile).start()
+    flags.wait()
+    for tile in range(tiles):
+        bring(tile).wait()
+        for member in range(2):
+            valid = mask_ref[member] != 0
+            for var in range(VARS):
+                for col in range(COLS):
+                    low = col * LANES
+                    high = min(low + LANES, GRID_LON)
+                    piece = held[member * VARS + var, tile * 8 : tile * 8 + 8, low:high]
+                    if high - low < LANES:
+                        fill = jnp.zeros((8, LANES - (high - low)), jnp.float32)
+                        piece = jnp.concatenate([piece, fill], axis=1)
+                    piece = jnp.where(valid, piece, PAD)
+                    start = tile * depth + slot(member, var * COLS + col)
+                    packed[pl.ds(start, 8, stride=BLOCK), :] = piece
+        take(tile).start()
+    for tile in range(tiles):
+        take(tile).wait()
 
 
 def pack(ensemble, valid_mask):
     rows = ensemble.shape[3]
-    flat = ensemble.reshape(2 * VARS, rows, GRID_LON)
     packed = pl.pallas_call(
         pack_kernel,
-        grid=(rows // 8,),
-        in_specs=[
-            pl.BlockSpec(memory_space=pltpu.SMEM),
-            pl.BlockSpec((2 * VARS, 8, GRID_LON), lambda t: (0, t, 0)),
-        ],
-        out_specs=pl.BlockSpec((8 * BLOCK, LANES), lambda t: (t, 0)),
+        in_specs=[pl.BlockSpec(memory_space=pltpu.HBM)] * 2,
+        out_specs=pl.BlockSpec(memory_space=pltpu.HBM),
         out_shape=jax.ShapeDtypeStruct((rows * BLOCK, LANES), jnp.float32),
+        scratch_shapes=[
+            pltpu.SMEM((2,), jnp.int32),
+            pltpu.VMEM((2 * VARS, rows, GRID_LON), jnp.float32),
+            pltpu.VMEM((rows * BLOCK, LANES), jnp.float32),
+            pltpu.SemaphoreType.DMA((rows // 8 + 1,)),
+            pltpu.SemaphoreType.DMA((rows // 8,)),
+        ],
+        compiler_params=pltpu.CompilerParams(vmem_limit_bytes=VMEM_LIMIT),
         name="pack",
-    )(valid_mask, flat)
+    )(in_hbm(valid_mask), in_hbm(ensemble.reshape(2 * VARS, rows, GRID_LON)))
     return packed.reshape(rows, BLOCK, LANES)
 
 
-def truth_kernel(row_ref, in_ref, out_ref):
-    mine = lax.broadcasted_iota(jnp.int32, (8, LANES), 0) == row_ref[0] % 8
-    out_ref[...] = jnp.zeros(out_ref.shape, jnp.float32)
+def truth_kernel(start_ref, in_ref, truth_ref, weight_ref, near, arrived):
+    row = position()
+    around = pl.ds(pl.multiple_of((row // 8) * 8, 8), 8)
+    look = pltpu.make_async_copy(in_ref.at[:, around, :], near, arrived)
+    look.start()
+    place = jnp.full((8, LANES), start_ref[0] + row, jnp.int32).astype(jnp.float32)
+    angle = (90.0 - place * 180.0 / (GRID_LAT - 1)) * math.pi / 180.0
+    weight_ref[...] = jnp.cos(angle)
+    mine = lax.broadcasted_iota(jnp.int32, (8, LANES), 0) == row % 8
+    truth_ref[...] = jnp.zeros(truth_ref.shape, jnp.float32)
+    look.wait()
     for var in range(VARS):
         for col in range(COLS):
             low = col * LANES
             high = min(low + LANES, GRID_LON)
-            piece = jnp.where(mine[:, : high - low], in_ref[var, :, low:high], 0.0)
-            row = var * COLS + col
-            out_ref[row : row + 1, : high - low] = jnp.sum(piece, axis=0, keepdims=True)
-
-
-def truth(observation, row):
-    flat = observation.reshape(VARS, observation.shape[2], GRID_LON)
+            piece = jnp.where(mine[:, : high - low], near[var, :, low:high], 0.0)
+            to = var * COLS + col
+            truth_ref[to : to + 1, : high - low] = jnp.sum(piece, axis=0, keepdims=True)
+
+
+def truth(observation, band_start):
+    rows = observation.shape[2]
     return pl.pallas_call(
         truth_kernel,
-        grid_spec=pltpu.PrefetchScalarGridSpec(
-            num_scalar_prefetch=1,
-            grid=(1,),
-            in_specs=[pl.BlockSpec((VARS, 8, GRID_LON), lambda i, where: (0, where[0] // 8, 0))],
-            out_specs=pl.BlockSpec((40, LANES), lambda i, where: (0, 0)),
-        ),
-        out_shape=jax.ShapeDtypeStruct((40, LANES), jnp.float32),
+        in_specs=[
+            pl.BlockSpec(memory_space=pltpu.SMEM),
+            pl.BlockSpec(memory_space=pltpu.HBM),
+        ],
+        out_specs=[pl.BlockSpec(memory_space=pltpu.VMEM)] * 2,
+        out_shape=[
+            jax.ShapeDtypeStruct((40, LANES), jnp.float32),
+            jax.ShapeDtypeStruct((8, LANES), jnp.float32),
+        ],
+        scratch_shapes=[
+            pltpu.VMEM((VARS, 8, GRID_LON), jnp.float32),
+            pltpu.SemaphoreType.DMA(()),
+        ],
         compiler_params=pltpu.CompilerParams(vmem_limit_bytes=VMEM_LIMIT),
         name="truth",
-    )(row.reshape(1), flat)
+    )(band_start, in_hbm(observation.reshape(VARS, rows, GRID_LON)))
 
 
 def compare(values, i, j):
@@ -171,14 +220,14 @@
             total = total + row
         total = jnp.sum(total, axis=1, keepdims=True)
         sums = jnp.where(lane == var, total, sums)
-    sums_ref[...] = jnp.broadcast_to(sums * weight_ref[0], sums_ref.shape)
+    sums_ref[...] = jnp.broadcast_to(sums * weight_ref[0:1, :], sums_ref.shape)
 
 
 def score(weight, members, observed, copies):
     return pl.pallas_call(
         score_kernel,
         in_specs=[
-            pl.BlockSpec(memory_space=pltpu.SMEM),
+            pl.BlockSpec(memory_space=pltpu.VMEM),
             pl.BlockSpec(memory_space=pltpu.VMEM),
             pl.BlockSpec(memory_space=pltpu.VMEM),
         ],
@@ -193,20 +242,41 @@
     )(weight, members, observed)
 
 
+def finish_kernel(in_ref, ready_ref, table_ref, field_ref, table, sent, *, cells):
+    first = pltpu.make_async_copy(ready_ref, field_ref, sent.at[0])
+    second = pltpu.make_async_copy(table, table_ref, sent.at[1])
+    first.start()
+    table[...] = jnp.sum(in_ref[...], axis=0, keepdims=True)[:, :VARS] / cells
+    second.start()
+    first.wait()
+    second.wait()
+
+
+def finish(sums, field, cells):
+    return pl.pallas_call(
+        functools.partial(finish_kernel, cells=cells),
+        in_specs=[pl.BlockSpec(memory_space=pltpu.VMEM)] * 2,
+        out_specs=[pl.BlockSpec(memory_space=pltpu.HBM)] * 2,
+        out_shape=[
+            jax.ShapeDtypeStruct((1, VARS), jnp.float32),
+            jax.ShapeDtypeStruct(field.shape, jnp.float32),
+        ],
+        scratch_shapes=[pltpu.VMEM((1, VARS), jnp.float32), pltpu.SemaphoreType.DMA((2,))],
+        compiler_params=pltpu.CompilerParams(vmem_limit_bytes=VMEM_LIMIT),
+        name="finish",
+    )(sums, field)
+
+
 def on_device(ensemble, observation, valid_mask, band_start):
     lat_rows = ensemble.shape[3]
-    row = lax.axis_index(MEMBER).astype(jnp.int32)
     packed = pack(ensemble, valid_mask)
     members = lax.all_to_all(packed, MEMBER, split_axis=0, concat_axis=0, tiled=True)
-    observed = truth(observation, row)
-    place = (band_start + row).astype(jnp.float32)
-    weight = jnp.cos((90.0 - place * 180.0 / (GRID_LAT - 1)) * math.pi / 180.0)
-    copies = lax.axis_size(MEMBER_LAT)
-    field, sums = score(weight, members, observed, copies)
+    observed, weight = truth(observation, band_start)
+    field, sums = score(weight, members, observed, lax.axis_size(MEMBER_LAT))
     sums = lax.all_to_all(sums, MEMBER_LAT, split_axis=0, concat_axis=0, tiled=True)
-    total = jnp.sum(sums, axis=0)[:VARS].reshape(VARS, 1)
-    score_table = total / (lax.axis_size("lat") * lat_rows * GRID_LON)
-    return (field.reshape(VARS, 1, 1, GRID_LON), score_table)
+    cells = lax.axis_size("lat") * lat_rows * GRID_LON
+    table, field = finish(sums, field, cells)
+    return (field.reshape(VARS, 1, 1, GRID_LON), table.reshape(VARS, 1))
 
 
 def solution(mesh):

time: 50 us -> 47.9 us (0.958)
  waiting for transfers between devices: 17.6 us -> 16.7 us
  other arithmetic: 0.67 us -> 0 us
    all_to_all x1, waiting for transfers between devices: 17.6 us -> 16.7 us  [on_device(): lax.all_to_all(packed, MEMBER, split_axis=0, concat_axis=0, tiled=True)]
    div x1 -> x0, other arithmetic: 0.52 us -> none  [on_device(): score_table = total / (lax.axis_size('lat') * lat_rows * GRID_LON)]
    pallas_call x3 -> x4, Pallas kernels: 5.05 us -> 4.71 us  [the longest x1 2.12 us: pack(): pl.pallas_call(pack_kernel, in_specs=[pl.BlockSpec(memory_space=pltpu.HBM...]
  transfers between devices with their start and end apart: 1 -> 1, of which waited for: 1 -> 1; matrix products, arithmetic and copies ran while one was open for 0% -> 0% of each run, Pallas kernels for 0% -> 2%
where the time goes in v2:
time: 47.9 us; the launch traced here: 47.6 us
  waiting for transfers between devices  16.7 us (35%)
  blocking collectives  16.3 us (34%)
  starting transfers between devices  8.59 us (18%)
  Pallas kernels  4.71 us (10%)
  between operations  1.3 us (3%)
    all_to_all x1, waiting for transfers between devices, on_device(): lax.all_to_all(packed, MEMBER, split_axis=0, concat_axis=0, tiled=True)  16.7 us
    all_to_all x1, blocking collectives, on_device(): lax.all_to_all(sums, MEMBER_LAT, split_axis=0, concat_axis=0, tiled=True)  16.3 us
    all_to_all x1, starting transfers between devices, on_device(): lax.all_to_all(packed, MEMBER, split_axis=0, concat_axis=0, tiled=True)  8.59 us
    pallas_call x1, Pallas kernels, pack(): pl.pallas_call(pack_kernel, in_specs=[pl.BlockSpec(memory_space=pltpu.HBM...  2.12 us
    pallas_call x1, Pallas kernels, truth(): pl.pallas_call(truth_kernel, in_specs=[pl.BlockSpec(memory_space=pltpu.SM...  0.98 us
    pallas_call x1, Pallas kernels, score(): pl.pallas_call(score_kernel, in_specs=[pl.BlockSpec(memory_space=pltpu.VM...  0.98 us
  transfers between devices with their start and end apart: 1, of which 1 were waited for; matrix products, arithmetic and copies ran while one was open for 0% of the time, Pallas kernels for 2%

profile of v2, /device:TPU:1, one launch (start us, length us, event | category | flops | bytes accessed | tf_op | source)
XLA Modules:
  0.0 47.6 jit_solution(18212514725939203120)
XLA Ops:
  0.6 2.1 %pack.1 = f32[2304,128]{1,0:T(8,128)} custom-call(s32[2]{0:T(128)} %mask_in.1, f32[6,32,1440]{2,1,0:T(8,128)} %bitcast.13), custom_call_target="tpu_custom_call" | custom-call | tf_op jit(solution)/shard_map/pack/pallas_call | solution.py:81
  2.8 8.6 %all-to-all-start = ((f32[32,72,128]{2,1,0:T(8,128)}), f32[32,72,128]{2,1,0:T(8,128)S(1)}, u32[]{:S(2)}, u32[]{:S(2)}) async-start(f32[32,72,128]{2,1,0:T(8,128)} %bitcast.2), calls=%async_computation | async-start | bytes 2359296 | tf_op jit(solution)/shard_map/all_to_all | solution.py:273
  12.0 1.0 %truth.1 = (f32[40,128]{1,0:T(8,128)S(1)}, f32[8,128]{1,0:T(8,128)S(1)}) custom-call(s32[1]{0:T(128)S(6)} %copy.9.start_ref, f32[3,32,1440]{2,1,0:T(8,128)} %bitcast.14), custom_call_target="tpu_custom_call" | custom-call | tf_op jit(solution)/shard_map/truth/pallas_call | solution.py:121
  13.0 16.7 %all-to-all-done.in_ref = f32[32,72,128]{2,1,0:T(8,128)S(1)} async-done(((f32[32,72,128]{2,1,0:T(8,128)}), f32[32,72,128]{2,1,0:T(8,128)S(1)}, u32[]{:S(2)}, u32[]{:S(2)}) %all-to-all-start) | async-done | bytes 1179680 | tf_op jit(solution)/shard_map/all_to_all | solution.py:273
  29.7 1.0 %score.1 = (f32[3,1,1440]{2,1,0:T(1,128)S(1)}, f32[128,128]{1,0:T(8,128)S(1)}) custom-call(f32[8,128]{1,0:T(8,128)S(1)} %get-tuple-element.8.weight_ref, f32[32,72,128]{2,1,0:T(8,128)S(1)} %all-to-all-done.in_ref, f32[40,128]{1,0:T(8,128)S(1)} %get-tuple-element.9.truth_ref), custom_call_target="tpu_custom_call" | custom-call | tf_op jit(solution)/shard_map/score/pallas_call | solution.py:227
  30.7 16.3 %all_to_all.16 = f32[128,1,128]{2,1,0:T(1,128)S(1)} all-to-all(f32[128,1,128]{2,1,0:T(1,128)S(1)} %bitcast.12), channel_id=1, replica_groups=mesh['member_0'=4,'member_1'=4,'member_2'=2,'lat'=4] {'member_0','member..., dimensions={0} | all-to-all | bytes 131072 | tf_op jit(solution)/shard_map/all_to_all | solution.py:276
  47.0 0.6 %finish.1 = (f32[1,3]{1,0:T(1,128)}, f32[3,1,1440]{2,1,0:T(1,128)}) custom-call(f32[128,128]{1,0:T(8,128)S(1)} %bitcast.11, f32[3,1,1440]{2,1,0:T(1,128)S(1)} %get-tuple-element.11.ready_ref), custom_call_target="tpu_custom_call" | custom-call | tf_op jit(solution)/shard_map/finish/pallas_call | solution.py:256
Async XLA Ops:
  2.8 27.0 %all-to-all-start = ((f32[32,72,128]{2,1,0:T(8,128)}), f32[32,72,128]{2,1,0:T(8,128)S(1)}, u32[]{:S(2)}, u32[]{:S(2)}) async-start(f32[32,72,128]{2,1,0:T(8,128)} %bitcast.2), calls=%async_computation | async-start | bytes 2359296 | tf_op jit(solution)/shard_map/all_to_all | solution.py:273

commit v3 on v2

--- a/solution.py
+++ b/solution.py
@@ -12,10 +12,11 @@
 GRID_LAT = 721
 GRID_LON = 1440
 LANES = 128
-COLS = 12
 VARS = 3
-ROWS = 36
-BLOCK = 72
+FULL = 11
+TAIL = 32
+BLOCK = 68
+WHOLE = 32
 MEMBERS = 64
 VALID = 50
 VMEM_LIMIT = 8 * 2**20
@@ -25,10 +26,6 @@
 LAT_MEMBER = ("lat", "member_0", "member_1", "member_2")
 
 
-def slot(member, row):
-    return 32 * member + row if row < 32 else 64 + 4 * member + row - 32
-
-
 def position():
     return lax.axis_index(MEMBER).astype(jnp.int32)
 
@@ -40,6 +37,7 @@
 def pack_kernel(mask_in, in_ref, out_ref, mask_ref, held, packed, arrived, left):
     tiles = held.shape[1] // 8
     depth = 8 * BLOCK
+    core = lax.axis_index(MEMBER[2]).astype(jnp.int32)
 
     def bring(tile):
         rows = pl.ds(tile * 8, 8)
@@ -58,19 +56,25 @@
     flags.wait()
     for tile in range(tiles):
         bring(tile).wait()
+        rows = slice(tile * 8, tile * 8 + 8)
         for member in range(2):
             valid = mask_ref[member] != 0
+            pieces = []
+            ends = []
             for var in range(VARS):
-                for col in range(COLS):
+                for col in range(FULL):
                     low = col * LANES
-                    high = min(low + LANES, GRID_LON)
-                    piece = held[member * VARS + var, tile * 8 : tile * 8 + 8, low:high]
-                    if high - low < LANES:
-                        fill = jnp.zeros((8, LANES - (high - low)), jnp.float32)
-                        piece = jnp.concatenate([piece, fill], axis=1)
-                    piece = jnp.where(valid, piece, PAD)
-                    start = tile * depth + slot(member, var * COLS + col)
-                    packed[pl.ds(start, 8, stride=BLOCK), :] = piece
+                    pieces.append(held[member * VARS + var, rows, low : low + LANES])
+                ends.append(held[member * VARS + var, rows, FULL * LANES : GRID_LON])
+            ends.append(jnp.zeros((8, LANES - VARS * TAIL), jnp.float32))
+            pieces.append(jnp.concatenate(ends, axis=1))
+            for row, piece in enumerate(pieces):
+                piece = jnp.where(valid, piece, PAD)
+                if row < WHOLE:
+                    start = tile * depth + 4 * core + WHOLE * member + row
+                else:
+                    start = tile * depth + 64 * (1 - core) + 2 * member + row - WHOLE
+                packed[pl.ds(start, 8, stride=BLOCK), :] = piece
         take(tile).start()
     for tile in range(tiles):
         take(tile).wait()
@@ -93,7 +97,7 @@
         compiler_params=pltpu.CompilerParams(vmem_limit_bytes=VMEM_LIMIT),
         name="pack",
     )(in_hbm(valid_mask), in_hbm(ensemble.reshape(2 * VARS, rows, GRID_LON)))
-    return packed.reshape(rows, BLOCK, LANES)
+    return packed.reshape(rows, BLOCK // 4, 4, LANES)
 
 
 def truth_kernel(start_ref, in_ref, truth_ref, weight_ref, near, arrived):
@@ -105,15 +109,22 @@
     angle = (90.0 - place * 180.0 / (GRID_LAT - 1)) * math.pi / 180.0
     weight_ref[...] = jnp.cos(angle)
     mine = lax.broadcasted_iota(jnp.int32, (8, LANES), 0) == row % 8
-    truth_ref[...] = jnp.zeros(truth_ref.shape, jnp.float32)
     look.wait()
-    for var in range(VARS):
-        for col in range(COLS):
-            low = col * LANES
-            high = min(low + LANES, GRID_LON)
-            piece = jnp.where(mine[:, : high - low], near[var, :, low:high], 0.0)
-            to = var * COLS + col
-            truth_ref[to : to + 1, : high - low] = jnp.sum(piece, axis=0, keepdims=True)
+
+    def pick(var, low, high):
+        piece = jnp.where(mine[:, : high - low], near[var, :, low:high], 0.0)
+        return jnp.sum(piece, axis=0, keepdims=True)
+
+    rows = [
+        pick(var, col * LANES, col * LANES + LANES) for var in range(VARS) for col in range(FULL)
+    ]
+    ends = [pick(var, FULL * LANES, GRID_LON) for var in range(VARS)]
+    ends.append(jnp.zeros((1, LANES - VARS * TAIL), jnp.float32))
+    rows.append(jnp.concatenate(ends, axis=1))
+    for row in range(WHOLE):
+        truth_ref[row : row + 1, :] = rows[row]
+    for row in range(8):
+        truth_ref[WHOLE + row : WHOLE + row + 1, :] = rows[WHOLE + row % 2]
 
 
 def truth(observation, band_start):
@@ -171,53 +182,79 @@
     return skill * (1.0 / VALID) - spread * (1.0 / (VALID * (VALID - 1.0)))
 
 
-def score_kernel(weight_ref, in_ref, truth_ref, field_ref, sums_ref, field):
-    @pl.loop(0, 4)
-    def _(tile):
-        start = pl.multiple_of(tile * 8, 8)
-        values = []
-        for source in range(MEMBERS // 2):
-            values.append(in_ref[source, pl.ds(start, 8), :])
-            values.append(in_ref[source, pl.ds(32 + start, 8), :])
-        sort(values, list(range(MEMBERS)))
-        field[pl.ds(start, 8), :] = score_of(values[:VALID], truth_ref[pl.ds(start, 8), :])
-
-    half = MEMBERS // 2
-    values = [in_ref[source, 64:72, :] for source in range(half)]
-    sort(values, list(range(half)))
-    upper = lax.broadcasted_iota(jnp.int32, (8, LANES), 0) >= 4
-    other = [pltpu.roll(v, 4, 0) for v in values]
-    values = [
-        jnp.where(
-            upper,
-            jnp.maximum(values[k], other[half - 1 - k]),
-            jnp.minimum(values[k], other[half - 1 - k]),
-        )
-        for k in range(half)
-    ]
-    step = half // 2
+def halve(values):
+    step = len(values) // 2
     while step:
-        for k in range(half):
+        for k in range(len(values)):
             if not k & step:
                 compare(values, k, k + step)
         step //= 2
-    above = [pltpu.roll(v, 4, 0) for v in values[: VALID - half]]
-    field[32:40, :] = score_of(values + above, truth_ref[32:40, :])
+
+
+def score_rest(parts, observed):
+    count = len(parts)
+    sublane = lax.broadcasted_iota(jnp.int32, (8, LANES), 0)
+    pair = sublane // 2
+    odd = pair % 2 == 1
+    upper = pair >= 2
+    values = list(parts)
+
+    def swap(v, beside):
+        up, down = pltpu.roll(v, 2, 0), pltpu.roll(v, 6, 0)
+        return jnp.where(odd, up, down) if beside else jnp.where(odd, down, up)
+
+    def split(values, others, high):
+        return [
+            jnp.where(high, jnp.maximum(v, w), jnp.minimum(v, w)) for v, w in zip(values, others)
+        ]
+
+    sort(values, list(range(count)))
+    values = split(values, [swap(v, True) for v in values[::-1]], odd)
+    halve(values)
+    values = split(values, [swap(v, False) for v in values[::-1]], upper)
+    values = split(values, [swap(v, True) for v in values], odd)
+    halve(values)
+    skill = jnp.zeros((8, LANES), jnp.float32)
+    spread = jnp.zeros((8, LANES), jnp.float32)
+    for k, v in enumerate(values):
+        rank = count * pair + k
+        v = jnp.where(rank < VALID, v, observed)
+        weight = jnp.where(rank < VALID, 2 * rank - (VALID - 1), 0).astype(jnp.float32)
+        skill = skill + jnp.abs(v - observed)
+        spread = spread + weight * v
+    total = skill * (1.0 / VALID) - spread * (1.0 / (VALID * (VALID - 1.0)))
+    total = total + pltpu.roll(total, 4, 0)
+    return total + pltpu.roll(total, 2, 0)
+
+
+def score_kernel(weight_ref, in_ref, truth_ref, field_ref, sums_ref, field):
+    sources = MEMBERS // 2
+
+    @pl.loop(0, WHOLE // 8)
+    def _(tile):
+        values = []
+        for source in range(sources):
+            for member in range(2):
+                base = BLOCK * source + 4 * (source % 2) + WHOLE * member
+                at = pl.multiple_of(base + tile * 8, 8)
+                values.append(in_ref[pl.ds(at, 8), :])
+        sort(values, list(range(MEMBERS)))
+        start = pl.multiple_of(tile * 8, 8)
+        field[pl.ds(start, 8), :] = score_of(values[:VALID], truth_ref[pl.ds(start, 8), :])
+
+    parts = [in_ref[136 * k + 64 : 136 * k + 72, :] for k in range(sources // 2)]
+    field[WHOLE : WHOLE + 8, :] = score_rest(parts, truth_ref[WHOLE : WHOLE + 8, :])
 
     lane = lax.broadcasted_iota(jnp.int32, (1, LANES), 1)
-    last = GRID_LON - (COLS - 1) * LANES
+    ends = field[VARS * FULL : VARS * FULL + 1, :]
     sums = jnp.zeros((1, LANES), jnp.float32)
     for var in range(VARS):
-        total = jnp.zeros((1, LANES), jnp.float32)
-        for col in range(COLS):
-            row = field[var * COLS + col : var * COLS + col + 1, :]
-            low = col * LANES
-            if col == COLS - 1:
-                field_ref[var, :, low:GRID_LON] = row[:, :last]
-                row = jnp.where(lane < last, row, 0.0)
-            else:
-                field_ref[var, :, low : low + LANES] = row
+        total = jnp.where((lane >= var * TAIL) & (lane < (var + 1) * TAIL), ends, 0.0)
+        for col in range(FULL):
+            row = field[var * FULL + col : var * FULL + col + 1, :]
+            field_ref[var, :, col * LANES : col * LANES + LANES] = row
             total = total + row
+        field_ref[var, :, FULL * LANES : GRID_LON] = ends[:, var * TAIL : (var + 1) * TAIL]
         total = jnp.sum(total, axis=1, keepdims=True)
         sums = jnp.where(lane == var, total, sums)
     sums_ref[...] = jnp.broadcast_to(sums * weight_ref[0:1, :], sums_ref.shape)
@@ -271,6 +308,7 @@
     lat_rows = ensemble.shape[3]
     packed = pack(ensemble, valid_mask)
     members = lax.all_to_all(packed, MEMBER, split_axis=0, concat_axis=0, tiled=True)
+    members = members.reshape(-1, LANES)
     observed, weight = truth(observation, band_start)
     field, sums = score(weight, members, observed, lax.axis_size(MEMBER_LAT))
     sums = lax.all_to_all(sums, MEMBER_LAT, split_axis=0, concat_axis=0, tiled=True)

time: 47.9 us -> 47.2 us (0.985)
  waiting for transfers between devices: 16.7 us -> 16 us
    all_to_all x1, waiting for transfers between devices: 16.7 us -> 16 us  [on_device(): lax.all_to_all(packed, MEMBER, split_axis=0, concat_axis=0, tiled=True)]
where the time goes in v3:
time: 47.2 us; the launch traced here: 46.9 us
  blocking collectives  16.3 us (35%)
  waiting for transfers between devices  16 us (34%)
  starting transfers between devices  8.59 us (18%)
  Pallas kernels  4.69 us (10%)
  between operations  1.3 us (3%)
    all_to_all x1, blocking collectives, on_device(): lax.all_to_all(sums, MEMBER_LAT, split_axis=0, concat_axis=0, tiled=True)  16.3 us
    all_to_all x1, waiting for transfers between devices, on_device(): lax.all_to_all(packed, MEMBER, split_axis=0, concat_axis=0, tiled=True)  16 us
    all_to_all x1, starting transfers between devices, on_device(): lax.all_to_all(packed, MEMBER, split_axis=0, concat_axis=0, tiled=True)  8.59 us
    pallas_call x1, Pallas kernels, pack(): pl.pallas_call(pack_kernel, in_specs=[pl.BlockSpec(memory_space=pltpu.HBM...  2.11 us
    pallas_call x1, Pallas kernels, truth(): pl.pallas_call(truth_kernel, in_specs=[pl.BlockSpec(memory_space=pltpu.SM...  1.02 us
  transfers between devices with their start and end apart: 1, of which 1 were waited for; matrix products, arithmetic and copies ran while one was open for 0% of the time, Pallas kernels for 2%

profile of v3, /device:TPU:1, one launch (start us, length us, event | category | flops | bytes accessed | tf_op | source)
XLA Modules:
  0.0 46.9 jit_solution(3445583776625456595)
XLA Ops:
  0.6 2.1 %pack.1 = f32[2176,128]{1,0:T(8,128)} custom-call(s32[2]{0:T(128)} %mask_in.1, f32[6,32,1440]{2,1,0:T(8,128)} %bitcast.15), custom_call_target="tpu_custom_call" | custom-call | tf_op jit(solution)/shard_map/pack/pallas_call | solution.py:85
  2.7 8.6 %all-to-all-start = ((f32[32,17,4,128]{3,2,1,0:T(4,128)}), f32[32,17,4,128]{3,2,1,0:T(4,128)S(1)}, u32[]{:S(2)}, u32[]{:S(2)}) async-start(f32[32,17,4,128]{3,2,1,0:T(4,128)} %bitcast.2), calls=%async_computation | async-start | bytes 2228224 | tf_op jit(solution)/shard_map/all_to_all | solution.py:310
  12.0 1.0 %truth.1 = (f32[40,128]{1,0:T(8,128)S(1)}, f32[8,128]{1,0:T(8,128)S(1)}) custom-call(s32[1]{0:T(128)S(6)} %copy.9.start_ref, f32[3,32,1440]{2,1,0:T(8,128)} %bitcast.16), custom_call_target="tpu_custom_call" | custom-call | tf_op jit(solution)/shard_map/truth/pallas_call | solution.py:132
  13.0 16.0 %all-to-all-done = f32[32,17,4,128]{3,2,1,0:T(4,128)S(1)} async-done(((f32[32,17,4,128]{3,2,1,0:T(4,128)}), f32[32,17,4,128]{3,2,1,0:T(4,128)S(1)}, u32[]{:S(2)}, u32[]{:S(2)}) %all-to-all-start) | async-done | bytes 1114144 | tf_op jit(solution)/shard_map/all_to_all | solution.py:310
  29.0 0.9 %score.1 = (f32[3,1,1440]{2,1,0:T(1,128)S(1)}, f32[128,128]{1,0:T(8,128)S(1)}) custom-call(f32[8,128]{1,0:T(8,128)S(1)} %get-tuple-element.8.weight_ref, f32[2176,128]{1,0:T(8,128)S(1)} %bitcast.12, f32[40,128]{1,0:T(8,128)S(1)} %get-tuple-element.9.truth_ref), custom_call_target="tpu_custom_call" | custom-call | tf_op jit(solution)/shard_map/score/pallas_call | solution.py:264
  29.9 16.3 %all_to_all.16 = f32[128,1,128]{2,1,0:T(1,128)S(1)} all-to-all(f32[128,1,128]{2,1,0:T(1,128)S(1)} %bitcast.14), channel_id=1, replica_groups=mesh['member_0'=4,'member_1'=4,'member_2'=2,'lat'=4] {'member_0','member..., dimensions={0} | all-to-all | bytes 131072 | tf_op jit(solution)/shard_map/all_to_all | solution.py:314
  46.2 0.6 %finish.1 = (f32[1,3]{1,0:T(1,128)}, f32[3,1,1440]{2,1,0:T(1,128)}) custom-call(f32[128,128]{1,0:T(8,128)S(1)} %bitcast.13, f32[3,1,1440]{2,1,0:T(1,128)S(1)} %get-tuple-element.11.ready_ref), custom_call_target="tpu_custom_call" | custom-call | tf_op jit(solution)/shard_map/finish/pallas_call | solution.py:293
Async XLA Ops:
  2.7 26.2 %all-to-all-start = ((f32[32,17,4,128]{3,2,1,0:T(4,128)}), f32[32,17,4,128]{3,2,1,0:T(4,128)S(1)}, u32[]{:S(2)}, u32[]{:S(2)}) async-start(f32[32,17,4,128]{3,2,1,0:T(4,128)} %bitcast.2), calls=%async_computation | async-start | bytes 2228224 | tf_op jit(solution)/shard_map/all_to_all | solution.py:310

commit v4 on v3

--- a/solution.py
+++ b/solution.py
@@ -22,7 +22,7 @@
 VMEM_LIMIT = 8 * 2**20
 PAD = 1e30
 MEMBER = ("member_0", "member_1", "member_2")
-MEMBER_LAT = ("member_0", "member_1", "member_2", "lat")
+MEMBER_LAT = ("member_2", "member_0", "member_1", "lat")
 LAT_MEMBER = ("lat", "member_0", "member_1", "member_2")
 
 

time: 47.2 us -> 46.8 us (level)
  no operation moved by 1% of the time
where the time goes in v4:
time: 46.8 us; the launch traced here: 46.5 us
  waiting for transfers between devices  16 us (34%)
  blocking collectives  16 us (34%)
  starting transfers between devices  8.59 us (18%)
  Pallas kernels  4.69 us (10%)
  between operations  1.3 us (3%)
    all_to_all x1, blocking collectives, on_device(): lax.all_to_all(sums, MEMBER_LAT, split_axis=0, concat_axis=0, tiled=True)  16 us
    all_to_all x1, waiting for transfers between devices, on_device(): lax.all_to_all(packed, MEMBER, split_axis=0, concat_axis=0, tiled=True)  16 us
    all_to_all x1, starting transfers between devices, on_device(): lax.all_to_all(packed, MEMBER, split_axis=0, concat_axis=0, tiled=True)  8.59 us
    pallas_call x1, Pallas kernels, pack(): pl.pallas_call(pack_kernel, in_specs=[pl.BlockSpec(memory_space=pltpu.HBM...  2.11 us
    pallas_call x1, Pallas kernels, truth(): pl.pallas_call(truth_kernel, in_specs=[pl.BlockSpec(memory_space=pltpu.SM...  1.02 us
  transfers between devices with their start and end apart: 1, of which 1 were waited for; matrix products, arithmetic and copies ran while one was open for 0% of the time, Pallas kernels for 2%

profile of v4, /device:TPU:1, one launch (start us, length us, event | category | flops | bytes accessed | tf_op | source)
XLA Modules:
  0.0 46.5 jit_solution(6000174796437728052)
XLA Ops:
  0.6 2.1 %pack.1 = f32[2176,128]{1,0:T(8,128)} custom-call(s32[2]{0:T(128)} %mask_in.1, f32[6,32,1440]{2,1,0:T(8,128)} %bitcast.15), custom_call_target="tpu_custom_call" | custom-call | tf_op jit(solution)/shard_map/pack/pallas_call | solution.py:85
  2.7 8.6 %all-to-all-start = ((f32[32,17,4,128]{3,2,1,0:T(4,128)}), f32[32,17,4,128]{3,2,1,0:T(4,128)S(1)}, u32[]{:S(2)}, u32[]{:S(2)}) async-start(f32[32,17,4,128]{3,2,1,0:T(4,128)} %bitcast.2), calls=%async_computation | async-start | bytes 2228224 | tf_op jit(solution)/shard_map/all_to_all | solution.py:310
  12.0 1.0 %truth.1 = (f32[40,128]{1,0:T(8,128)S(1)}, f32[8,128]{1,0:T(8,128)S(1)}) custom-call(s32[1]{0:T(128)S(6)} %copy.9.start_ref, f32[3,32,1440]{2,1,0:T(8,128)} %bitcast.16), custom_call_target="tpu_custom_call" | custom-call | tf_op jit(solution)/shard_map/truth/pallas_call | solution.py:132
  13.0 16.0 %all-to-all-done = f32[32,17,4,128]{3,2,1,0:T(4,128)S(1)} async-done(((f32[32,17,4,128]{3,2,1,0:T(4,128)}), f32[32,17,4,128]{3,2,1,0:T(4,128)S(1)}, u32[]{:S(2)}, u32[]{:S(2)}) %all-to-all-start) | async-done | bytes 1114144 | tf_op jit(solution)/shard_map/all_to_all | solution.py:310
  29.0 0.9 %score.1 = (f32[3,1,1440]{2,1,0:T(1,128)S(1)}, f32[128,128]{1,0:T(8,128)S(1)}) custom-call(f32[8,128]{1,0:T(8,128)S(1)} %get-tuple-element.8.weight_ref, f32[2176,128]{1,0:T(8,128)S(1)} %bitcast.12, f32[40,128]{1,0:T(8,128)S(1)} %get-tuple-element.9.truth_ref), custom_call_target="tpu_custom_call" | custom-call | tf_op jit(solution)/shard_map/score/pallas_call | solution.py:264
  29.9 16.0 %all_to_all.16 = f32[128,1,128]{2,1,0:T(1,128)S(1)} all-to-all(f32[128,1,128]{2,1,0:T(1,128)S(1)} %bitcast.14), channel_id=1, replica_groups=mesh['member_0'=4,'member_1'=4,'member_2'=2,'lat'=4] {'member_2','member..., dimensions={0} | all-to-all | bytes 131072 | tf_op jit(solution)/shard_map/all_to_all | solution.py:314
  45.9 0.6 %finish.1 = (f32[1,3]{1,0:T(1,128)}, f32[3,1,1440]{2,1,0:T(1,128)}) custom-call(f32[128,128]{1,0:T(8,128)S(1)} %bitcast.13, f32[3,1,1440]{2,1,0:T(1,128)S(1)} %get-tuple-element.11.ready_ref), custom_call_target="tpu_custom_call" | custom-call | tf_op jit(solution)/shard_map/finish/pallas_call | solution.py:293
Async XLA Ops:
  2.7 26.2 %all-to-all-start = ((f32[32,17,4,128]{3,2,1,0:T(4,128)}), f32[32,17,4,128]{3,2,1,0:T(4,128)S(1)}, u32[]{:S(2)}, u32[]{:S(2)}) async-start(f32[32,17,4,128]{3,2,1,0:T(4,128)} %bitcast.2), calls=%async_computation | async-start | bytes 2228224 | tf_op jit(solution)/shard_map/all_to_all | solution.py:310
